TPU v7x, 32 devices: a whole 2x2x4 slice. The times are simulated.
32 devices in a mesh: patch: 32 (over z, y, x, core).
Axes of the slice: x: 2, y: 2, z: 4, core: 2. Of those that a mesh axis runs over, the one named last changes fastest.
Arguments:
- positions: float32 [3, 65536], P(None, 'patch'), may hold values from -6 to 6
- densities: float32 [3, 65536], P(None, 'patch'), may hold values from -6 to 6
- near_src: int32 [512, 8], P('patch'), may hold values from 0 to 511, as said below
- near_count: int32 [512], P('patch'), may hold values from 1 to 8
- far_slot: int32 [512, 32], P('patch'), may hold values from 0 to 127
- far_class: int32 [512, 32], P('patch'), may hold values from 0 to 188
- far_count: int32 [512], P('patch'), may hold values from 1 to 32
- requests: int32 [32, 32, 4], P('patch'), may hold values from 0 to 15, as said below
- up_basis: bfloat16 [512, 144, 384], P('patch'), may hold values from -0.3125 to 0.3125
- transfer_table: bfloat16 [189, 20736], replicated, may hold values from -0.5 to 0.5
- down_basis: bfloat16 [512, 144, 9, 128], P('patch'), may hold values from -0.09375 to 0.09375
Outputs:
- shape_grad: float32 [3, 65536], P(None, 'patch')
Inputs may be any that keep to these rules, and one draw needn't show every extreme that they name: `near_src`: the source leaf of each near-field block is held by the device of its target leaf or by the device just before or after it along patch. `requests`: each row names 4 different leaves of the source device, by their index on that device.
All inputs are finite; a program needn't handle non-finite values.
Results may differ from a plain program's by a relative error of at most 0.0042.
Values may be sent and summed in bfloat16 or wider, within the bound.
A program may use at most 192 MiB of HBM per device.

v0:
```python
import functools
import math

import jax
import jax.numpy as jnp
from jax import lax
from jax.experimental import pallas as pl
from jax.experimental.pallas import tpu as pltpu
from jax.sharding import PartitionSpec as P

KERNEL = 1.0 / (8.0 * math.pi)
BLOB = 0.25
MESH = pl.DeviceIdType.MESH
F32 = jnp.float32
BF16 = jnp.bfloat16


def iota(shape, dim):
    return lax.broadcasted_iota(jnp.int32, shape, dim)


def dot(a, b):
    return jnp.dot(a, b, preferred_element_type=F32)


def exchange(
    n,
    pos,
    dens,
    up_hbm,
    pos_b,
    pos_a,
    dens_b,
    dens_a,
    mom,
    up,
    dens_rows,
    local_sem,
    halo_send,
    halo_recv,
):
    leaves, width = mom.shape
    size = pos.shape[1] // leaves
    me = lax.axis_index("patch")
    right = lax.rem(me + 1, n)
    left = lax.rem(me + n - 1, n)
    get_up = pltpu.make_async_copy(up_hbm, up, local_sem)
    get_up.start()
    barrier = pltpu.get_barrier_semaphore()

    for peer in (left, right):
        pl.semaphore_signal(barrier, inc=1, device_id=(peer,), device_id_type=MESH)

    for leaf in range(leaves):
        for c in range(3):
            dens_rows[leaf : leaf + 1, c * size : (c + 1) * size] = dens[
                c : c + 1, leaf * size : (leaf + 1) * size
            ]
    dens_round = dens_rows[...].astype(BF16)
    pl.semaphore_wait(barrier, 2)
    halos = []
    for k, (src, dst, peer) in enumerate(
        ((pos, pos_b, right), (dens, dens_b, right), (pos, pos_a, left), (dens, dens_a, left))
    ):
        copy = pltpu.make_async_remote_copy(
            src_ref=src,
            dst_ref=dst,
            send_sem=halo_send.at[k],
            recv_sem=halo_recv.at[k],
            device_id=(peer,),
            device_id_type=MESH,
        )
        copy.start()
        halos.append(copy)

    get_up.wait()
    row = iota((leaves, width), 0)
    total = jnp.zeros((leaves, width), F32)
    for leaf in range(leaves):
        got = lax.dot_general(
            dens_round, up[leaf], (((1,), (1,)), ((), ())), preferred_element_type=F32
        )
        total = total + jnp.where(row == leaf, got, 0.0)
    mom[...] = total.astype(BF16)

    for copy in halos:
        copy.wait()


def near_field(
    near_src,
    near_count,
    first,
    pos,
    dens,
    pos_b,
    pos_a,
    dens_b,
    dens_a,
    near,
    part_b,
    part_a,
    window,
    tb,
    tacc,
    near_t,
    src_acc,
):
    leaves = near_count.shape[0]
    size = pos.shape[1] // leaves
    src_acc[...] = jnp.zeros_like(src_acc)
    window[...] = jnp.zeros_like(window)
    for part, (x, f) in enumerate(((pos_b, dens_b), (pos, dens), (pos_a, dens_a))):
        for leaf in range(leaves):
            lanes = slice(leaf * size, (leaf + 1) * size)
            window[part * leaves + leaf, 0:3, :] = x[:, lanes]
            window[part * leaves + leaf, 3:6, :] = f[:, lanes]

    offset = first[0]
    lane = iota((size, size), 1)

    @pl.loop(0, leaves)
    def _(leaf):
        columns = jnp.transpose(window[leaves + leaf])
        for c in range(6):
            col = columns[:, c : c + 1]
            if c >= 3:
                col = col * KERNEL
            tb[c] = jnp.broadcast_to(col, (size, size))
        tacc[...] = jnp.zeros_like(tacc)

        def near_block(slot, carry):
            index = near_src[slot, leaf] - offset
            other = window[index]
            xs = [jnp.broadcast_to(other[c : c + 1], (8, size)) for c in range(3)]
            fs = [jnp.broadcast_to(other[c : c + 1], (8, size)) for c in range(3, 6)]
            src_sum = [None] * 3
            for g in range(size // 8):
                r8 = slice(g * 8, (g + 1) * 8)
                ft = [tb[3 + c, r8, :] for c in range(3)]
                sep = [tb[c, r8, :] - xs[c] for c in range(3)]
                rho = sep[0] * sep[0] + sep[1] * sep[1] + sep[2] * sep[2] + BLOB
                inv1 = lax.rsqrt(rho)
                inv2 = inv1 * inv1
                inv3 = inv1 * inv2
                ab = ft[0] * fs[0] + ft[1] * fs[1] + ft[2] * fs[2]
                ar = ft[0] * sep[0] + ft[1] * sep[1] + ft[2] * sep[2]
                br = fs[0] * sep[0] + fs[1] * sep[1] + fs[2] * sep[2]
                p = br * inv3
                q = ar * inv3
                w = ab * inv3 + (3.0 * (p * ar)) * inv2
                for c in range(3):
                    t = ft[c] * p + fs[c] * q - w * sep[c]
                    tacc[c, r8, :] += t
                    src_sum[c] = t if g == 0 else src_sum[c] + t
            for c in range(3):
                src_acc[index, c] += src_sum[c]
            return carry

        lax.fori_loop(0, near_count[leaf], near_block, 0)
        cols = [jnp.sum(tacc[c], axis=1, keepdims=True) for c in range(3)]
        mixed = jnp.where(lane == 0, cols[0], jnp.where(lane == 1, cols[1], cols[2]))
        near_t[leaf] = jnp.transpose(mixed)[0:8]

    for part, buf in ((0, part_b), (2, part_a)):
        for leaf in range(leaves):
            for c in range(3):
                buf[c : c + 1, leaf * size : (leaf + 1) * size] = jnp.sum(
                    src_acc[part * leaves + leaf, c], axis=0, keepdims=True
                )
    for leaf in range(leaves):
        for c in range(3):
            near[c : c + 1, leaf * size : (leaf + 1) * size] = near_t[
                leaf, c : c + 1, :
            ] - jnp.sum(src_acc[leaves + leaf, c], axis=0, keepdims=True)


def far_field(
    n,
    far_count,
    dens,
    far_slot,
    far_class,
    req,
    mom_own,
    near,
    part_b,
    part_a,
    table_hbm,
    down_hbm,
    out,
    mom,
    got_b,
    got_a,
    table,
    down,
    hot_class,
    hot_slot,
    tiled,
    sums,
    fold,
    expan,
    far_acc,
    table_sem,
    down_sem,
    mom_send,
    mom_recv,
    part_send,
    part_recv,
):
    leaves, width = mom_own.shape
    me = lax.axis_index("patch")
    barrier = pltpu.get_barrier_semaphore()

    @pl.loop(1, n)
    def _(k):
        pl.semaphore_signal(
            barrier, inc=1, device_id=(lax.rem(me + k, n),), device_id_type=MESH
        )

    size = dens.shape[1] // leaves
    far_num = far_slot.shape[1]
    classes = table.shape[0]
    cap = req.shape[0]
    block = fold.shape[0]

    def table_copy(b):
        lanes = pl.ds(pl.multiple_of(b * block, 128), block)
        return pltpu.make_async_copy(
            table_hbm.at[:, lanes], table.at[:, lanes], table_sem.at[b]
        )

    for b in range(width * width // block):
        table_copy(b).start()
    get_down = pltpu.make_async_copy(down_hbm, down, down_sem)
    get_down.start()
    count_col = jnp.zeros((leaves, 1), jnp.int32)
    leaf_col = iota((leaves, 1), 0)
    for leaf in range(leaves):
        count_col = jnp.where(leaf_col == leaf, far_count[leaf], count_col)
    class_iota = iota((leaves, classes), 1)
    for s in range(far_num):
        rows = slice(s * leaves, (s + 1) * leaves)
        wanted = jnp.where(s < count_col, far_class[:, s : s + 1], -1)
        hot_class[rows, :] = (class_iota == wanted).astype(F32).astype(BF16)
    fold_row = iota(fold.shape, 0)
    fold_first = iota(fold.shape, 1) * width
    fold[...] = (
        ((fold_row >= fold_first) & (fold_row < fold_first + width)).astype(F32).astype(BF16)
    )
    pl.semaphore_wait(barrier, n - 1)

    def mom_copy(k):
        return pltpu.make_async_remote_copy(
            src_ref=mom_own,
            dst_ref=mom.at[me],
            send_sem=mom_send.at[k],
            recv_sem=mom_recv.at[k],
            device_id=(lax.rem(me + k, n),),
            device_id_type=MESH,
        )

    @pl.loop(1, n)
    def _(k):
        mom_copy(k).start()

    parts = []
    for k, (src, dst, peer) in enumerate(
        (
            (part_b, got_a, lax.rem(me + n - 1, n)),
            (part_a, got_b, lax.rem(me + 1, n)),
        )
    ):
        copy = pltpu.make_async_remote_copy(
            src_ref=src,
            dst_ref=dst,
            send_sem=part_send.at[k],
            recv_sem=part_recv.at[k],
            device_id=(peer,),
            device_id_type=MESH,
        )
        copy.start()
        parts.append(copy)

    mom[me] = mom_own[...]
    column = iota((leaves, cap * n), 1)
    slot_of = lax.rem(column, n) * cap + lax.div(column, n)
    for s in range(far_num):
        rows = slice(s * leaves, (s + 1) * leaves)
        slot = far_slot[:, s : s + 1]
        hot_slot[rows, :] = (slot_of == slot).astype(F32).astype(BF16)
    period = tiled.shape[1]
    spread_gap = iota((width, period), 1) - iota((width, period), 0)
    spread = spread_gap == 0
    for k in range(1, period // width):
        spread = spread | (spread_gap == k * width)
    spread = spread.astype(F32).astype(BF16)

    @pl.loop(1, n)
    def _(k):
        mom_copy(k).wait_recv()

    moments = mom[...].reshape(n * leaves, width)
    leaf_iota = iota((n * leaves, n), 0) - iota((n * leaves, n), 1) * leaves
    picked = []
    for place in range(cap):
        pick = (leaf_iota == req[place : place + 1, :]).astype(F32).astype(BF16)
        chosen = lax.dot_general(
            pick, moments, (((0,), (0,)), ((), ())), preferred_element_type=F32
        ).astype(BF16)
        picked.append(dot(chosen, spread).astype(BF16))
    chosen_rows = jnp.concatenate(picked, axis=0)
    for k in range(period // 128):
        lanes = slice(k * 128, (k + 1) * 128)
        tiled[:, lanes] = dot(hot_slot[...], chosen_rows[:, lanes])

    expan[...] = jnp.zeros_like(expan)
    step = 256 if block % 256 == 0 else 128
    per_block = block // width

    @pl.loop(0, width * width // block)
    def _(b):
        table_copy(b).wait()
        for t in range(block // step):
            start = pl.multiple_of(b * block + t * step, 128)
            oper = dot(hot_class[...], table[:, pl.ds(start, step)])
            for h in range(step // 128):
                at = ((t * step) // 128 + h) % (period // 128)
                acc = None
                for s in range(far_num):
                    rows = slice(s * leaves, (s + 1) * leaves)
                    term = oper[rows, h * 128 : (h + 1) * 128] * tiled[
                        rows, at * 128 : (at + 1) * 128
                    ]
                    acc = term if acc is None else acc + term
                sums[:, t * step + h * 128 : t * step + (h + 1) * 128] = acc
        whole = sums[...]
        high = whole.astype(BF16)
        low = (whole - high.astype(F32)).astype(BF16)
        res = dot(high, fold[...]) + dot(low, fold[...])
        wide = jnp.concatenate([res, jnp.zeros((leaves, expan.shape[1] - 128), F32)], axis=1)
        expan[...] += pltpu.roll(wide, b * per_block, 1)

    expansion = expan[...][:, :width].astype(BF16)
    get_down.wait()
    far_acc[...] = jnp.zeros_like(far_acc)
    leaf_row = iota((leaves, size), 0)

    @pl.loop(0, leaves)
    def _(leaf):
        lanes = pl.ds(pl.multiple_of(leaf * size, size), size)
        own = dens[:, lanes]
        fields = [dot(expansion, down[leaf, q]) for q in range(9)]
        for k in range(3):
            far = (
                own[0:1] * fields[k] + own[1:2] * fields[3 + k] + own[2:3] * fields[6 + k]
            )
            far_acc[k] += jnp.where(leaf_row == leaf, far, 0.0)

    for copy in parts:
        copy.wait_recv()
    for leaf in range(leaves):
        lanes = slice(leaf * size, (leaf + 1) * size)
        for c in range(3):
            came = got_b[c : c + 1, lanes] + got_a[c : c + 1, lanes]
            out[c : c + 1, lanes] = near[c : c + 1, lanes] - came + far_acc[c, leaf : leaf + 1, :]
    for copy in parts:
        copy.wait_send()

    @pl.loop(1, n)
    def _(k):
        mom_copy(k).wait_send()


def per_device(
    n,
    positions,
    densities,
    near_src,
    near_count,
    far_slot,
    far_class,
    far_count,
    requests,
    up_basis,
    transfer_table,
    down_basis,
):
    leaves = near_count.shape[0]
    nodes = positions.shape[1]
    size = nodes // leaves
    width = up_basis.shape[1]
    far_num = far_slot.shape[1]
    cap = requests.shape[2]
    classes = transfer_table.shape[0]
    period = math.lcm(width, 128)
    blocks = width * width // period
    block = 2 * period if blocks % 2 == 0 else period
    down = jnp.transpose(down_basis, (0, 2, 1, 3))
    blocks = width * width // block
    smem = pl.BlockSpec(memory_space=pltpu.SMEM)
    vmem = pl.BlockSpec(memory_space=pltpu.VMEM)
    hbm = pl.BlockSpec(memory_space=pl.ANY)
    line = jax.ShapeDtypeStruct((3, nodes), F32)
    limit = 60 * 1024 * 1024
    pos_b, pos_a, dens_b, dens_a, mom = pl.pallas_call(
        functools.partial(exchange, n),
        out_shape=[line] * 4 + [jax.ShapeDtypeStruct((leaves, width), BF16)],
        in_specs=[vmem] * 2 + [hbm],
        out_specs=[vmem] * 5,
        scratch_shapes=[
            pltpu.VMEM(up_basis.shape, BF16),
            pltpu.VMEM((leaves, 3 * size), F32),
            pltpu.SemaphoreType.DMA,
            pltpu.SemaphoreType.DMA((4,)),
            pltpu.SemaphoreType.DMA((4,)),
        ],
        compiler_params=pltpu.CompilerParams(
            collective_id=0, has_side_effects=True, vmem_limit_bytes=limit
        ),
    )(positions, densities, up_basis)
    first = ((lax.axis_index("patch") - 1) * leaves).reshape(1)
    near, part_b, part_a = pl.pallas_call(
        near_field,
        out_shape=[line] * 3,
        in_specs=[smem] * 3 + [vmem] * 6,
        out_specs=[vmem] * 3,
        scratch_shapes=[
            pltpu.VMEM((3 * leaves, 8, size), F32),
            pltpu.VMEM((6, size, size), F32),
            pltpu.VMEM((3, size, size), F32),
            pltpu.VMEM((leaves, 8, size), F32),
            pltpu.VMEM((3 * leaves, 3, 8, size), F32),
        ],
        compiler_params=pltpu.CompilerParams(vmem_limit_bytes=limit),
    )(near_src.T, near_count, first, positions, densities, pos_b, pos_a, dens_b, dens_a)
    return pl.pallas_call(
        functools.partial(far_field, n),
        out_shape=line,
        in_specs=[smem] + [vmem] * 8 + [hbm] * 2,
        out_specs=vmem,
        scratch_shapes=[
            pltpu.VMEM((n, leaves, width), BF16),
            pltpu.VMEM((3, nodes), F32),
            pltpu.VMEM((3, nodes), F32),
            pltpu.VMEM(transfer_table.shape, BF16),
            pltpu.VMEM(down.shape, BF16),
            pltpu.VMEM((far_num * leaves, classes), BF16),
            pltpu.VMEM((far_num * leaves, cap * n), BF16),
            pltpu.VMEM((far_num * leaves, period), F32),
            pltpu.VMEM((leaves, block), F32),
            pltpu.VMEM((block, 128), BF16),
            pltpu.VMEM((leaves, (width + 127) // 128 * 128), F32),
            pltpu.VMEM((3, leaves, size), F32),
            pltpu.SemaphoreType.DMA((blocks,)),
            pltpu.SemaphoreType.DMA,
            pltpu.SemaphoreType.DMA((n,)),
            pltpu.SemaphoreType.DMA((n,)),
            pltpu.SemaphoreType.DMA((2,)),
            pltpu.SemaphoreType.DMA((2,)),
        ],
        compiler_params=pltpu.CompilerParams(
            collective_id=1, has_side_effects=True, vmem_limit_bytes=limit
        ),
    )(
        far_count,
        densities,
        far_slot,
        far_class,
        requests[0].T,
        mom,
        near,
        part_b,
        part_a,
        transfer_table,
        down,
    )


def solution(mesh):
    placed = (
        P(None, "patch"),
        P(None, "patch"),
        P("patch", None),
        P("patch"),
        P("patch", None),
        P("patch", None),
        P("patch"),
        P("patch", None, None),
        P("patch", None, None),
        P(),
        P("patch", None, None, None),
    )
    return jax.shard_map(
        functools.partial(per_device, mesh.shape["patch"]),
        mesh=mesh,
        in_specs=placed,
        out_specs=P(None, "patch"),
        check_vma=False,
    )
```

profile of v0, /device:TPU:0, one launch (start us, length us, event | category | flops | bytes accessed | tf_op | source)
XLA Modules:
  0.0 54.3 jit_solution(5068716474508892839)
XLA Ops:
  0.0 10.5 %shard_map.109 = (f32[3,2048]{1,0:T(4,128)}, f32[3,2048]{1,0:T(4,128)}, f32[3,2048]{1,0:T(4,128)}, f32[3,2048]{1,0:T(4,128)}, bf16[16,144]{1,0:T(8,128)(2,1)}) custom-call(f32[3,2048]{1,0:T(4,128)} %pos.3, f32[3,2048]{1,0:T(4,128)} %dens.5, bf16[16,144,384]{2,1,0:T(8,128)(2,1)} %up_hbm.1), custom_call_target="tpu_custom_call" | custom-call | tf_op jit(solution)/shard_map/pallas_call | solution.py:406
  10.5 15.4 %shard_map.110 = (f32[3,2048]{1,0:T(4,128)}, f32[3,2048]{1,0:T(4,128)}, f32[3,2048]{1,0:T(4,128)}) custom-call(s32[8,16]{1,0:T(8,128)} %bitcast.7, s32[16]{0:T(128)} %near_count.1, s32[1]{0:T(128)} %bitcast.3.first, f32[3,2048]{1,0:T(4,128)} %pos.3, f32[3,2048]{1,0:T(4,128)} %dens.5, f32[3,2048]{1,0:T(4,128)} %get-tuple-element.14.pos_b, ...), custom_call_target="tpu_custom_call" | custom-call | tf_op jit(solution)/shard_map/pallas_call | solution.py:423
  26.0 27.0 %shard_map.111 = f32[3,2048]{1,0:T(4,128)} custom-call(s32[16]{0:T(128)} %far_count.1, f32[3,2048]{1,0:T(4,128)} %dens.5, s32[16,32]{1,0:T(8,128)} %far_slot.1, s32[16,32]{1,0:T(8,128)} %far_class.1, s32[4,32]{1,0:T(4,128)} %bitcast.8, bf16[16,144]{1,0:T(8,128)(2,1)} %get-tuple-element.13.mom_own, f32[3,2048]{1,0:T(4,128)} %get-tuple-element.18.near, ...), custom_call_target="tpu_custom_call" | custom-call | tf_op jit(solution)/shard_map/pallas_call | solution.py:437
  53.0 1.4 %copy.13 = f32[3,2048]{1,0:T(4,128)} copy(f32[3,2048]{1,0:T(4,128)} %shard_map.111) | data formatting | bytes 49152
where the time goes:
time: 55.4 us; the launch traced here: 54.3 us
  Pallas kernels  52.9 us (95%)
  local copies, waits for them, and re-layouts  1.38 us (2%)
    pallas_call x1, Pallas kernels, per_device(): pl.pallas_call(functools.partial(far_field, n), out_shape=line, in_specs=...  27 us
    pallas_call x1, Pallas kernels, per_device(): pl.pallas_call(near_field, out_shape=[line] * 3, in_specs=[smem] * 3 + [v...  15.4 us
    pallas_call x1, Pallas kernels, per_device(): pl.pallas_call(functools.partial(exchange, n), out_shape=[line] * 4 + [ja...  10.5 us
    unnamed x1, local copies, waits for them, and re-layouts  1.38 us

commit v1 on v0

v1 whole, which is shorter than its diff:
```python
import functools
import math

import jax
import jax.numpy as jnp
import numpy as np
from jax import lax
from jax.experimental import pallas as pl
from jax.experimental.pallas import tpu as pltpu
from jax.sharding import PartitionSpec as P

KERNEL = 1.0 / (8.0 * math.pi)
BLOB = 0.25
MESH = pl.DeviceIdType.MESH
F32 = jnp.float32
BF16 = jnp.bfloat16

ROWS = 48
FEATURES = 48
LEFT = (0, 0, 0, 1, 1, 2)
RIGHT = (0, 1, 2, 0, 1, 0)


def at(group):
    return (group // 2) * 8 + (group % 2) * 3


def source_choice():
    sel = np.zeros((4, FEATURES, ROWS), np.float32)
    for k in range(6):
        for c in range(3):
            sel[0, 3 * k + c, at(3 + RIGHT[k]) + c] = 1.0
            sel[1, 3 * k + c, at(6 + RIGHT[k]) + c] = -1.0
            sel[2, 18 + 3 * k + c, at(RIGHT[k]) + c] = 1.0
            sel[3, 18 + 3 * k + c, at(6 + RIGHT[k]) + c] = -2.0
    for c in range(3):
        sel[1, 36 + c, at(11) + c] = 1.0
        sel[2, 42 + c, at(9) + c] = -1.0
        sel[3, 39 + c, at(11) + c] = 1.0
        sel[3, 42 + c, at(10) + c] = 1.0
    return sel.reshape(4 * FEATURES, ROWS)


def target_choice(size):
    sel = np.zeros((ROWS, 128), np.float32)
    spread = np.zeros((ROWS, 6, size), np.float32)
    for k in range(6):
        for c in range(3):
            sel[at(LEFT[k]) + c, 3 * k + c] = 1.0
            sel[at(3 + LEFT[k]) + c, 18 + 3 * k + c] = 1.0
    for c in range(3):
        sel[at(6) + c, 36 + c] = 1.0
        sel[at(7) + c, 39 + c] = 1.0
        sel[at(8) + c, 42 + c] = 1.0
        for piece in range(3):
            spread[at(3 + piece) + c, c, :] = 3.0
            spread[at(piece) + c, 3 + c, :] = 1.0
    return np.concatenate([sel, spread.reshape(ROWS, 6 * size)], axis=1)


def iota(shape, dim):
    return lax.broadcasted_iota(jnp.int32, shape, dim)


def dot(a, b):
    return jnp.dot(a, b, preferred_element_type=F32)


def pieces(x):
    high = x.astype(BF16).astype(F32)
    rest = x - high
    mid = rest.astype(BF16).astype(F32)
    return high, mid, rest - mid


def inner(a, b):
    return a[0:1] * b[0:1] + a[1:2] * b[1:2] + a[2:3] * b[2:3]


def put(rows, group, value):
    rows[at(group) : at(group) + value.shape[0], : value.shape[1]] = value


def put_pieces(rows, group, value):
    for k, piece in enumerate(pieces(value)):
        if value.shape[0] == 3:
            put(rows, group + k, piece)
        else:
            rows[at(group) + k : at(group) + k + 1, : value.shape[1]] = piece


def source_rows(rows, x, f):
    put_pieces(rows, 0, f)
    put_pieces(rows, 3, f * (1.0 / 3.0))
    put_pieces(rows, 6, x)
    put_pieces(rows, 9, inner(f, x))
    put_pieces(rows, 10, inner(x, x) + BLOB)
    put(rows, 11, jnp.ones_like(x))


def target_rows(rows, x, f):
    a = f * KERNEL
    put_pieces(rows, 0, a)
    put_pieces(rows, 3, x)
    put_pieces(rows, 6, inner(a, x))
    put_pieces(rows, 7, inner(x, x))
    put(rows, 8, jnp.ones_like(x))


def flip(me, bit):
    return me + bit - 2 * bit * lax.rem(lax.div(me, bit), 2)


def body(
    n,
    near_src,
    near_count,
    far_count,
    pos,
    dens,
    far_slot,
    far_class,
    req,
    choose_src,
    choose_tgt,
    up_hbm,
    table_hbm,
    down_hbm,
    out,
    pos_b,
    pos_a,
    dens_b,
    dens_a,
    up,
    table,
    down,
    dens_rows,
    mom,
    rows_own,
    rows_oth,
    window,
    rhs,
    lhs,
    tb,
    geo0,
    geo1,
    tacc,
    cols,
    src_rows,
    hot_src,
    part_b,
    part_a,
    got_b,
    got_a,
    hot_class,
    hot_slot,
    tiled,
    sums,
    fold,
    expan,
    field,
    up_sem,
    table_sem,
    down_sem,
    halo_send,
    halo_recv,
    mom_send,
    mom_recv,
    part_send,
    part_recv,
):
    leaves, width = mom.shape[1:]
    nodes = pos.shape[1]
    size = nodes // leaves
    slots = near_src.shape[0]
    far_num = far_slot.shape[1]
    classes = table.shape[0]
    cap = req.shape[0]
    block = fold.shape[0]
    phases = n.bit_length() - 1
    me = lax.axis_index("patch")
    has_left = me > 0
    has_right = me < n - 1
    barrier = pltpu.get_barrier_semaphore()

    def signal(peer):
        pl.semaphore_signal(barrier, inc=1, device_id=(peer,), device_id_type=MESH)

    for t in range(phases):
        signal(flip(me, n >> (t + 1)))

    @pl.when(has_left)
    def _():
        signal(me - 1)

    @pl.when(has_right)
    def _():
        signal(me + 1)

    get_up = pltpu.make_async_copy(up_hbm, up, up_sem)
    get_up.start()

    def table_copy(b):
        lanes = pl.ds(pl.multiple_of(b * block, 128), block)
        return pltpu.make_async_copy(
            table_hbm.at[:, lanes], table.at[:, lanes], table_sem.at[b]
        )

    for b in range(width * width // block):
        table_copy(b).start()
    get_down = pltpu.make_async_copy(down_hbm, down, down_sem)
    get_down.start()

    for leaf in range(leaves):
        for c in range(3):
            dens_rows[leaf : leaf + 1, c * size : (c + 1) * size] = dens[
                c : c + 1, leaf * size : (leaf + 1) * size
            ]
    dens_round = dens_rows[...].astype(BF16)
    get_up.wait()
    row = iota((leaves, width), 0)
    total = jnp.zeros((leaves, width), F32)
    for leaf in range(leaves):
        got = lax.dot_general(
            dens_round, up[leaf], (((1,), (1,)), ((), ())), preferred_element_type=F32
        )
        total = total + jnp.where(row == leaf, got, 0.0)
    mom[0] = total.astype(BF16)

    def halo(k, src, dst, peer):
        return pltpu.make_async_remote_copy(
            src_ref=src,
            dst_ref=dst,
            send_sem=halo_send.at[k],
            recv_sem=halo_recv.at[k],
            device_id=(peer,),
            device_id_type=MESH,
        )

    to_right = (halo(0, pos, pos_b, me + 1), halo(1, dens, dens_b, me + 1))
    to_left = (halo(2, pos, pos_a, me - 1), halo(3, dens, dens_a, me - 1))

    def gather(t):
        return pltpu.make_async_remote_copy(
            src_ref=mom.at[0 : 1 << t],
            dst_ref=mom.at[1 << t : 2 << t],
            send_sem=mom_send.at[t],
            recv_sem=mom_recv.at[t],
            device_id=(flip(me, n >> (t + 1)),),
            device_id_type=MESH,
        )

    pl.semaphore_wait(
        barrier, phases + has_left.astype(jnp.int32) + has_right.astype(jnp.int32)
    )

    @pl.when(has_right)
    def _():
        for copy in to_right:
            copy.start()

    @pl.when(has_left)
    def _():
        for copy in to_left:
            copy.start()

    gather(0).start()

    rows_own[...] = jnp.zeros_like(rows_own)
    rows_oth[...] = jnp.zeros_like(rows_oth)
    target_rows(rows_own, pos[...], dens[...])

    @pl.loop(0, leaves)
    def _(leaf):
        lanes = pl.ds(pl.multiple_of(leaf * size, size), size)
        turned = jnp.transpose(rows_own[:, lanes]).astype(BF16)
        lhs[leaf] = dot(turned, choose_tgt[:, :128]).astype(BF16)
        tb[leaf] = dot(turned, choose_tgt[:, 128:])

    def sources(part, rows, x, f):
        source_rows(rows, x[...], f[...])
        for leaf in range(leaves):
            lanes = slice(leaf * size, (leaf + 1) * size)
            window[part * leaves + leaf, 0:3, :] = x[:, lanes] * 3.0
            window[part * leaves + leaf, 3:6, :] = f[:, lanes]

        @pl.loop(0, leaves)
        def _(leaf):
            lanes = pl.ds(pl.multiple_of(leaf * size, size), size)
            chosen = dot(choose_src[...], rows[:, lanes].astype(BF16)).astype(BF16)
            for o in range(4):
                rhs[part * leaves + leaf, :, o * size : (o + 1) * size] = chosen[
                    o * FEATURES : (o + 1) * FEATURES
                ]

    window[...] = jnp.zeros_like(window)
    nothing = jnp.zeros((3, size), F32)
    source_rows(rows_oth, nothing, nothing)
    chosen = dot(choose_src[...], rows_oth[:, :size].astype(BF16)).astype(BF16)
    for o in range(4):
        rhs[3 * leaves, :, o * size : (o + 1) * size] = chosen[
            o * FEATURES : (o + 1) * FEATURES
        ]
    sources(1, rows_oth, pos, dens)

    count_col = jnp.zeros((leaves, 1), jnp.int32)
    leaf_col = iota((leaves, 1), 0)
    for leaf in range(leaves):
        count_col = jnp.where(leaf_col == leaf, far_count[leaf], count_col)
    class_iota = iota((leaves, classes), 1)
    column = iota((leaves, cap * n), 1)
    slot_of = lax.rem(column, n) * cap + lax.div(column, n)
    for s in range(far_num):
        rows = slice(s * leaves, (s + 1) * leaves)
        wanted = jnp.where(s < count_col, far_class[:, s : s + 1], -1)
        hot_class[rows, :] = (class_iota == wanted).astype(F32).astype(BF16)
        slot = far_slot[:, s : s + 1]
        hot_slot[rows, :] = (slot_of == slot).astype(F32).astype(BF16)
    fold_row = iota(fold.shape, 0)
    fold_first = iota(fold.shape, 1) * width
    fold[...] = (
        ((fold_row >= fold_first) & (fold_row < fold_first + width)).astype(F32).astype(BF16)
    )
    cols[...] = jnp.zeros_like(cols)

    @pl.when(has_left)
    def _():
        for copy in to_right:
            copy.wait_recv()

    @pl.when(jnp.logical_not(has_left))
    def _():
        pos_b[...] = jnp.zeros_like(pos_b)
        dens_b[...] = jnp.zeros_like(dens_b)

    sources(0, rows_oth, pos_b, dens_b)

    @pl.when(has_right)
    def _():
        for copy in to_left:
            copy.wait_recv()

    @pl.when(jnp.logical_not(has_right))
    def _():
        pos_a[...] = jnp.zeros_like(pos_a)
        dens_a[...] = jnp.zeros_like(dens_a)

    sources(2, rows_own, pos_a, dens_a)

    offset = (me - 1) * leaves
    lane8 = iota((8, size), 1)
    lane1 = iota((1, 128), 1)

    def source_of(leaf, slot):
        live = slot < near_count[leaf]
        return jnp.where(live, near_src[slot, leaf] - offset, 3 * leaves)

    def geometry(geo, leaf, first):
        for k in range(2):
            geo[k] = dot(lhs[leaf][:, :FEATURES], rhs[source_of(leaf, first + k)])

    geometry(geo0, 0, 0)
    pairs = slots // 2

    @pl.loop(0, leaves)
    def _(leaf):
        for t in range(1, phases):
            @pl.when(leaf == ((t - 1) * leaves) // max(phases - 1, 1))
            def _():
                gather(t - 1).wait_recv()
                gather(t).start()

        following = lax.rem(leaf + 1, leaves)
        for pair in range(pairs):
            geo, other = ((geo0, geo1), (geo1, geo0))[pair % 2]
            if pair + 1 < pairs:
                geometry(other, leaf, 2 * pair + 2)
            else:
                geometry(other, following, 0)
            xs, fs, sums_src = [], [], []
            for k in range(2):
                index = source_of(leaf, 2 * pair + k)
                nodes_k = window[index]
                xs.append([jnp.broadcast_to(nodes_k[c : c + 1], (8, size)) for c in range(3)])
                fs.append([jnp.broadcast_to(nodes_k[3 + c : 4 + c], (8, size)) for c in range(3)])
                sums_src.append([None] * 3)
                hot_src[leaf, 2 * pair + k : 2 * pair + k + 1, :] = (lane1 == index).astype(F32)
            for g in range(size // 8):
                r8 = slice(g * 8, (g + 1) * 8)
                total = [None] * 3
                for k in range(2):
                    ab, ar, br, rho = [
                        geo[k, r8, o * size : (o + 1) * size] for o in range(4)
                    ]
                    inv1 = lax.rsqrt(rho)
                    inv2 = inv1 * inv1
                    inv3 = inv1 * inv2
                    p = br * inv3
                    q = ar * inv3
                    w = ab * inv3 + (p * ar) * inv2
                    for c in range(3):
                        sep = tb[leaf, r8, c * size : (c + 1) * size] - xs[k][c]
                        a = tb[leaf, r8, (3 + c) * size : (4 + c) * size]
                        term = a * p + fs[k][c] * q - w * sep
                        sums_src[k][c] = term if g == 0 else sums_src[k][c] + term
                        total[c] = term if k == 0 else total[c] + term
                for c in range(3):
                    if pair > 0:
                        total[c] = total[c] + tacc[c, r8, :]
                    if pair + 1 < pairs:
                        tacc[c, r8, :] = total[c]
                    else:
                        col = jnp.sum(total[c], axis=1, keepdims=True)
                        cols[r8, :] = jnp.where(lane8 == c * leaves + leaf, col, cols[r8, :])
            for k in range(2):
                for c in range(3):
                    src_rows[leaf, 2 * pair + k : 2 * pair + k + 1, c * size : (c + 1) * size] = (
                        jnp.sum(sums_src[k][c], axis=0, keepdims=True)
                    )

    near_t = jnp.transpose(cols[...])
    hot = jnp.transpose(hot_src[...].reshape(leaves * slots, 128)).astype(BF16)
    values = src_rows[...].reshape(leaves * slots, 3 * size)
    scattered = None
    for piece in pieces(values):
        term = dot(hot, piece.astype(BF16))
        scattered = term if scattered is None else scattered + term
    part_b[...] = scattered[:leaves]
    part_a[...] = scattered[2 * leaves : 3 * leaves]
    own = scattered[leaves : 2 * leaves]
    near = [
        near_t[c * leaves : (c + 1) * leaves] - own[:, c * size : (c + 1) * size]
        for c in range(3)
    ]
    for c in range(3):
        field[9 + c] = near[c]

    def part(k, src, dst, peer):
        return pltpu.make_async_remote_copy(
            src_ref=src,
            dst_ref=dst,
            send_sem=part_send.at[k],
            recv_sem=part_recv.at[k],
            device_id=(peer,),
            device_id_type=MESH,
        )

    part_left = part(0, part_b, got_a, me - 1)
    part_right = part(1, part_a, got_b, me + 1)

    @pl.when(has_left)
    def _():
        part_left.start()

    @pl.when(has_right)
    def _():
        part_right.start()

    gather(phases - 1).wait_recv()
    period = tiled.shape[1]
    spread_gap = iota((width, period), 1) - iota((width, period), 0)
    spread = spread_gap == 0
    for k in range(1, period // width):
        spread = spread | (spread_gap == k * width)
    spread = spread.astype(F32).astype(BF16)
    moments = mom[...].reshape(n * leaves, width)
    device = iota((1, n), 1)
    place_of = jnp.zeros((1, n), jnp.int32)
    for t in range(phases):
        bit = n >> (t + 1)
        mine = lax.rem(lax.div(me, bit), 2)
        theirs = lax.rem(lax.div(device, bit), 2)
        place_of = place_of + (theirs + mine - 2 * theirs * mine) * (1 << t)
    row_iota = iota((n * leaves, n), 0)
    picked = []
    for place in range(cap):
        wanted = place_of * leaves + req[place : place + 1, :]
        pick = (row_iota == wanted).astype(F32).astype(BF16)
        chosen = lax.dot_general(
            pick, moments, (((0,), (0,)), ((), ())), preferred_element_type=F32
        ).astype(BF16)
        picked.append(dot(chosen, spread).astype(BF16))
    chosen_rows = jnp.concatenate(picked, axis=0)
    for k in range(period // 128):
        lanes = slice(k * 128, (k + 1) * 128)
        tiled[:, lanes] = dot(hot_slot[...], chosen_rows[:, lanes])

    expan[...] = jnp.zeros_like(expan)
    step = 256 if block % 256 == 0 else 128
    per_block = block // width

    @pl.loop(0, width * width // block)
    def _(b):
        table_copy(b).wait()
        for t in range(block // step):
            start = pl.multiple_of(b * block + t * step, 128)
            oper = dot(hot_class[...], table[:, pl.ds(start, step)])
            for h in range(step // 128):
                tile = ((t * step) // 128 + h) % (period // 128)
                acc = None
                for s in range(far_num):
                    rows = slice(s * leaves, (s + 1) * leaves)
                    term = oper[rows, h * 128 : (h + 1) * 128] * tiled[
                        rows, tile * 128 : (tile + 1) * 128
                    ]
                    acc = term if acc is None else acc + term
                sums[:, t * step + h * 128 : t * step + (h + 1) * 128] = acc
        whole = sums[...]
        high = whole.astype(BF16)
        low = (whole - high.astype(F32)).astype(BF16)
        res = dot(high, fold[...]) + dot(low, fold[...])
        wide = jnp.concatenate([res, jnp.zeros((leaves, expan.shape[1] - 128), F32)], axis=1)
        expan[...] += pltpu.roll(wide, b * per_block, 1)

    expansion = expan[...][:, :width].astype(BF16)
    get_down.wait()
    leaf_row = iota((leaves, size), 0)
    for q in range(9):
        field[q] = jnp.zeros((leaves, size), F32)

    @pl.loop(0, leaves)
    def _(leaf):
        for q in range(9):
            got = dot(expansion, down[leaf, q])
            field[q] += jnp.where(leaf_row == leaf, got, 0.0)

    @pl.when(has_right)
    def _():
        part_left.wait_recv()

    @pl.when(jnp.logical_not(has_right))
    def _():
        got_a[...] = jnp.zeros_like(got_a)

    @pl.when(has_left)
    def _():
        part_right.wait_recv()

    @pl.when(jnp.logical_not(has_left))
    def _():
        got_b[...] = jnp.zeros_like(got_b)

    for k in range(3):
        lanes = slice(k * size, (k + 1) * size)
        result = field[9 + k] - (got_b[:, lanes] + got_a[:, lanes])
        for c in range(3):
            result = result + dens_rows[:, c * size : (c + 1) * size] * field[3 * c + k]
        for leaf in range(leaves):
            out[k : k + 1, leaf * size : (leaf + 1) * size] = result[leaf : leaf + 1]

    @pl.when(has_right)
    def _():
        part_right.wait_send()
        for copy in to_right:
            copy.wait_send()

    @pl.when(has_left)
    def _():
        part_left.wait_send()
        for copy in to_left:
            copy.wait_send()

    for t in range(phases):
        gather(t).wait_send()


def per_device(
    n,
    positions,
    densities,
    near_src,
    near_count,
    far_slot,
    far_class,
    far_count,
    requests,
    up_basis,
    transfer_table,
    down_basis,
):
    leaves, slots = near_src.shape
    nodes = positions.shape[1]
    size = nodes // leaves
    width = up_basis.shape[1]
    far_num = far_slot.shape[1]
    cap = requests.shape[2]
    classes = transfer_table.shape[0]
    phases = n.bit_length() - 1
    period = math.lcm(width, 128)
    blocks = width * width // period
    block = 2 * period if blocks % 2 == 0 else period
    down = jnp.transpose(down_basis, (0, 2, 1, 3))
    blocks = width * width // block
    smem = pl.BlockSpec(memory_space=pltpu.SMEM)
    vmem = pl.BlockSpec(memory_space=pltpu.VMEM)
    hbm = pl.BlockSpec(memory_space=pl.ANY)
    line = pltpu.VMEM((3, nodes), F32)
    part = pltpu.VMEM((leaves, 3 * size), F32)
    return pl.pallas_call(
        functools.partial(body, n),
        out_shape=jax.ShapeDtypeStruct((3, nodes), F32),
        in_specs=[smem] * 3 + [vmem] * 7 + [hbm] * 3,
        out_specs=vmem,
        scratch_shapes=[line] * 4
        + [
            pltpu.VMEM(up_basis.shape, BF16),
            pltpu.VMEM(transfer_table.shape, BF16),
            pltpu.VMEM(down.shape, BF16),
            part,
            pltpu.VMEM((n, leaves, width), BF16),
            pltpu.VMEM((ROWS, nodes), F32),
            pltpu.VMEM((ROWS, nodes), F32),
            pltpu.VMEM((3 * leaves + 1, 8, size), F32),
            pltpu.VMEM((3 * leaves + 1, FEATURES, 4 * size), BF16),
            pltpu.VMEM((leaves, size, 128), BF16),
            pltpu.VMEM((leaves, size, 6 * size), F32),
            pltpu.VMEM((2, size, 4 * size), F32),
            pltpu.VMEM((2, size, 4 * size), F32),
            pltpu.VMEM((3, size, size), F32),
            pltpu.VMEM((size, 128), F32),
            pltpu.VMEM((leaves, slots, 3 * size), F32),
            pltpu.VMEM((leaves, slots, 128), F32),
            part,
            part,
            part,
            part,
            pltpu.VMEM((far_num * leaves, classes), BF16),
            pltpu.VMEM((far_num * leaves, cap * n), BF16),
            pltpu.VMEM((far_num * leaves, period), F32),
            pltpu.VMEM((leaves, block), F32),
            pltpu.VMEM((block, 128), BF16),
            pltpu.VMEM((leaves, (width + 127) // 128 * 128), F32),
            pltpu.VMEM((12, leaves, size), F32),
            pltpu.SemaphoreType.DMA,
            pltpu.SemaphoreType.DMA((blocks,)),
            pltpu.SemaphoreType.DMA,
            pltpu.SemaphoreType.DMA((4,)),
            pltpu.SemaphoreType.DMA((4,)),
            pltpu.SemaphoreType.DMA((phases,)),
            pltpu.SemaphoreType.DMA((phases,)),
            pltpu.SemaphoreType.DMA((2,)),
            pltpu.SemaphoreType.DMA((2,)),
        ],
        compiler_params=pltpu.CompilerParams(
            collective_id=0, has_side_effects=True, vmem_limit_bytes=60 * 1024 * 1024
        ),
    )(
        near_src.T,
        near_count,
        far_count,
        positions,
        densities,
        far_slot,
        far_class,
        requests[0].T,
        jnp.asarray(source_choice(), BF16),
        jnp.asarray(target_choice(size), BF16),
        up_basis,
        transfer_table,
        down,
    )


def solution(mesh):
    placed = (
        P(None, "patch"),
        P(None, "patch"),
        P("patch", None),
        P("patch"),
        P("patch", None),
        P("patch", None),
        P("patch"),
        P("patch", None, None),
        P("patch", None, None),
        P(),
        P("patch", None, None, None),
    )
    return jax.shard_map(
        functools.partial(per_device, mesh.shape["patch"]),
        mesh=mesh,
        in_specs=placed,
        out_specs=P(None, "patch"),
        check_vma=False,
    )
```

time: 55.4 us -> 51.5 us (0.930); the launches traced: 54.3 us -> 51.3 us
  Pallas kernels: 52.9 us -> 49.9 us
    pallas_call x3 -> x1, Pallas kernels: 52.9 us -> 49.9 us  [per_device(): pl.pallas_call(functools.partial(body, n), out_shape=jax.ShapeDtypeStruct...]
where the time goes in v1:
time: 51.5 us; the launch traced here: 51.3 us
  Pallas kernels  49.9 us (97%)
  local copies, waits for them, and re-layouts  1.38 us (3%)
    pallas_call x1, Pallas kernels, per_device(): pl.pallas_call(functools.partial(body, n), out_shape=jax.ShapeDtypeStruct...  49.9 us
    unnamed x1, local copies, waits for them, and re-layouts  1.38 us

profile of v1, /device:TPU:0, one launch (start us, length us, event | category | flops | bytes accessed | tf_op | source)
XLA Modules:
  0.0 51.3 jit_solution(5453935495505474312)
XLA Ops:
  0.0 49.9 %shard_map.127 = f32[3,2048]{1,0:T(4,128)} custom-call(s32[8,16]{1,0:T(8,128)} %bitcast.6, s32[16]{0:T(128)} %near_count.1, s32[16]{0:T(128)} %far_count.1, f32[3,2048]{1,0:T(4,128)} %pos.1, f32[3,2048]{1,0:T(4,128)} %dens.1, s32[16,32]{1,0:T(8,128)} %far_slot.1, s32[16,32]{1,0:T(8,128)} %far_class.1, s32[4,32]{1,0:T(4,128)} %bitcast.7, ...), custom_call_target="tpu_custom_call" | custom-call | tf_op jit(solution)/shard_map/pallas_call | solution.py:599
  49.9 1.4 %copy.15 = f32[3,2048]{1,0:T(4,128)} copy(f32[3,2048]{1,0:T(4,128)} %shard_map.127) | data formatting | bytes 49152

commit v2 on v1

--- a/solution.py
+++ b/solution.py
@@ -157,7 +157,9 @@
     tiled,
     sums,
     fold,
-    expan,
+    scatter,
+    pick,
+    spread,
     field,
     up_sem,
     table_sem,
@@ -178,6 +180,7 @@
     cap = req.shape[0]
     block = fold.shape[0]
     phases = n.bit_length() - 1
+    expan_width = (width + 127) // 128 * 128
     me = lax.axis_index("patch")
     has_left = me > 0
     has_right = me < n - 1
@@ -270,12 +273,20 @@
     rows_oth[...] = jnp.zeros_like(rows_oth)
     target_rows(rows_own, pos[...], dens[...])
 
-    @pl.loop(0, leaves)
-    def _(leaf):
-        lanes = pl.ds(pl.multiple_of(leaf * size, size), size)
-        turned = jnp.transpose(rows_own[:, lanes]).astype(BF16)
-        lhs[leaf] = dot(turned, choose_tgt[:, :128]).astype(BF16)
-        tb[leaf] = dot(turned, choose_tgt[:, 128:])
+    few = 4
+
+    @pl.loop(0, leaves // few)
+    def _(group):
+        turned = []
+        for k in range(few):
+            start = pl.multiple_of((group * few + k) * size, size)
+            turned.append(jnp.transpose(rows_own[:, pl.ds(start, size)]).astype(BF16))
+        turned = jnp.concatenate(turned, axis=0)
+        spread_out = dot(turned, choose_tgt[...])
+        for k in range(few):
+            mine = spread_out[k * size : (k + 1) * size]
+            lhs[group * few + k] = mine[:, :128].astype(BF16)
+            tb[group * few + k] = mine[:, 128:]
 
     def sources(part, rows, x, f):
         source_rows(rows, x[...], f[...])
@@ -284,14 +295,15 @@
             window[part * leaves + leaf, 0:3, :] = x[:, lanes] * 3.0
             window[part * leaves + leaf, 3:6, :] = f[:, lanes]
 
-        @pl.loop(0, leaves)
-        def _(leaf):
-            lanes = pl.ds(pl.multiple_of(leaf * size, size), size)
-            chosen = dot(choose_src[...], rows[:, lanes].astype(BF16)).astype(BF16)
-            for o in range(4):
-                rhs[part * leaves + leaf, :, o * size : (o + 1) * size] = chosen[
-                    o * FEATURES : (o + 1) * FEATURES
-                ]
+        for leaf in range(0, leaves, 2):
+            chosen = dot(
+                choose_src[...], rows[:, leaf * size : (leaf + 2) * size].astype(BF16)
+            ).astype(BF16)
+            for k in range(2):
+                for o in range(4):
+                    rhs[part * leaves + leaf + k, :, o * size : (o + 1) * size] = chosen[
+                        o * FEATURES : (o + 1) * FEATURES, k * size : (k + 1) * size
+                    ]
 
     window[...] = jnp.zeros_like(window)
     nothing = jnp.zeros((3, size), F32)
@@ -322,31 +334,6 @@
         ((fold_row >= fold_first) & (fold_row < fold_first + width)).astype(F32).astype(BF16)
     )
     cols[...] = jnp.zeros_like(cols)
-
-    @pl.when(has_left)
-    def _():
-        for copy in to_right:
-            copy.wait_recv()
-
-    @pl.when(jnp.logical_not(has_left))
-    def _():
-        pos_b[...] = jnp.zeros_like(pos_b)
-        dens_b[...] = jnp.zeros_like(dens_b)
-
-    sources(0, rows_oth, pos_b, dens_b)
-
-    @pl.when(has_right)
-    def _():
-        for copy in to_left:
-            copy.wait_recv()
-
-    @pl.when(jnp.logical_not(has_right))
-    def _():
-        pos_a[...] = jnp.zeros_like(pos_a)
-        dens_a[...] = jnp.zeros_like(dens_a)
-
-    sources(2, rows_own, pos_a, dens_a)
-
     offset = (me - 1) * leaves
     lane8 = iota((8, size), 1)
     lane1 = iota((1, 128), 1)
@@ -355,23 +342,78 @@
         live = slot < near_count[leaf]
         return jnp.where(live, near_src[slot, leaf] - offset, 3 * leaves)
 
+    for leaf in range(leaves):
+        for slot in range(slots):
+            hot_src[leaf, slot : slot + 1, :] = (lane1 == source_of(leaf, slot)).astype(F32)
+    scatter[...] = jnp.transpose(hot_src[...].reshape(leaves * slots, 128)).astype(BF16)
+
+    device = iota((1, n), 1)
+    place_of = jnp.zeros((1, n), jnp.int32)
+    for t in range(phases):
+        bit = n >> (t + 1)
+        mine = lax.rem(lax.div(me, bit), 2)
+        theirs = lax.rem(lax.div(device, bit), 2)
+        place_of = place_of + (theirs + mine - 2 * theirs * mine) * (1 << t)
+    row_iota = iota((n * leaves, n), 0)
+    wanted = jnp.concatenate(
+        [
+            (row_iota == place_of * leaves + req[place : place + 1, :]).astype(F32)
+            for place in range(cap)
+        ],
+        axis=1,
+    )
+    pick[...] = jnp.transpose(wanted).astype(BF16)
+    period = tiled.shape[1]
+    spread_gap = iota((width, period), 1) - iota((width, period), 0)
+    near_gap = spread_gap == 0
+    for k in range(1, period // width):
+        near_gap = near_gap | (spread_gap == k * width)
+    spread[...] = near_gap.astype(F32).astype(BF16)
+
+    @pl.when(has_left)
+    def _():
+        for copy in to_right:
+            copy.wait_recv()
+
+    @pl.when(jnp.logical_not(has_left))
+    def _():
+        pos_b[...] = jnp.zeros_like(pos_b)
+        dens_b[...] = jnp.zeros_like(dens_b)
+
+    sources(0, rows_oth, pos_b, dens_b)
+
+    @pl.when(has_right)
+    def _():
+        for copy in to_left:
+            copy.wait_recv()
+
+    @pl.when(jnp.logical_not(has_right))
+    def _():
+        pos_a[...] = jnp.zeros_like(pos_a)
+        dens_a[...] = jnp.zeros_like(dens_a)
+
+    sources(2, rows_own, pos_a, dens_a)
+
     def geometry(geo, leaf, first):
         for k in range(2):
             geo[k] = dot(lhs[leaf][:, :FEATURES], rhs[source_of(leaf, first + k)])
 
     geometry(geo0, 0, 0)
     pairs = slots // 2
-
-    @pl.loop(0, leaves)
-    def _(leaf):
+    together = 2
+
+    @pl.loop(0, leaves // together)
+    def _(turn):
         for t in range(1, phases):
-            @pl.when(leaf == ((t - 1) * leaves) // max(phases - 1, 1))
+            @pl.when(turn == ((t - 1) * (leaves // together)) // max(phases - 1, 1))
             def _():
                 gather(t - 1).wait_recv()
                 gather(t).start()
 
-        following = lax.rem(leaf + 1, leaves)
-        for pair in range(pairs):
+        for sub in range(together * pairs):
+            leaf = turn * together + sub // pairs
+            pair = sub % pairs
+            following = lax.rem(leaf + 1, leaves)
             geo, other = ((geo0, geo1), (geo1, geo0))[pair % 2]
             if pair + 1 < pairs:
                 geometry(other, leaf, 2 * pair + 2)
@@ -384,7 +426,6 @@
                 xs.append([jnp.broadcast_to(nodes_k[c : c + 1], (8, size)) for c in range(3)])
                 fs.append([jnp.broadcast_to(nodes_k[3 + c : 4 + c], (8, size)) for c in range(3)])
                 sums_src.append([None] * 3)
-                hot_src[leaf, 2 * pair + k : 2 * pair + k + 1, :] = (lane1 == index).astype(F32)
             for g in range(size // 8):
                 r8 = slice(g * 8, (g + 1) * 8)
                 total = [None] * 3
@@ -419,11 +460,10 @@
                     )
 
     near_t = jnp.transpose(cols[...])
-    hot = jnp.transpose(hot_src[...].reshape(leaves * slots, 128)).astype(BF16)
     values = src_rows[...].reshape(leaves * slots, 3 * size)
     scattered = None
     for piece in pieces(values):
-        term = dot(hot, piece.astype(BF16))
+        term = dot(scatter[...], piece.astype(BF16))
         scattered = term if scattered is None else scattered + term
     part_b[...] = scattered[:leaves]
     part_a[...] = scattered[2 * leaves : 3 * leaves]
@@ -457,72 +497,60 @@
         part_right.start()
 
     gather(phases - 1).wait_recv()
-    period = tiled.shape[1]
-    spread_gap = iota((width, period), 1) - iota((width, period), 0)
-    spread = spread_gap == 0
-    for k in range(1, period // width):
-        spread = spread | (spread_gap == k * width)
-    spread = spread.astype(F32).astype(BF16)
     moments = mom[...].reshape(n * leaves, width)
-    device = iota((1, n), 1)
-    place_of = jnp.zeros((1, n), jnp.int32)
-    for t in range(phases):
-        bit = n >> (t + 1)
-        mine = lax.rem(lax.div(me, bit), 2)
-        theirs = lax.rem(lax.div(device, bit), 2)
-        place_of = place_of + (theirs + mine - 2 * theirs * mine) * (1 << t)
-    row_iota = iota((n * leaves, n), 0)
-    picked = []
-    for place in range(cap):
-        wanted = place_of * leaves + req[place : place + 1, :]
-        pick = (row_iota == wanted).astype(F32).astype(BF16)
-        chosen = lax.dot_general(
-            pick, moments, (((0,), (0,)), ((), ())), preferred_element_type=F32
-        ).astype(BF16)
-        picked.append(dot(chosen, spread).astype(BF16))
-    chosen_rows = jnp.concatenate(picked, axis=0)
-    for k in range(period // 128):
-        lanes = slice(k * 128, (k + 1) * 128)
-        tiled[:, lanes] = dot(hot_slot[...], chosen_rows[:, lanes])
-
-    expan[...] = jnp.zeros_like(expan)
+    chosen = dot(pick[...], moments).astype(BF16)
+    chosen_rows = dot(chosen, spread[...]).astype(BF16)
+    tiled[...] = dot(hot_slot[...], chosen_rows)
+
     step = 256 if block % 256 == 0 else 128
     per_block = block // width
-
-    @pl.loop(0, width * width // block)
-    def _(b):
-        table_copy(b).wait()
-        for t in range(block // step):
-            start = pl.multiple_of(b * block + t * step, 128)
-            oper = dot(hot_class[...], table[:, pl.ds(start, step)])
-            for h in range(step // 128):
-                tile = ((t * step) // 128 + h) % (period // 128)
-                acc = None
-                for s in range(far_num):
-                    rows = slice(s * leaves, (s + 1) * leaves)
-                    term = oper[rows, h * 128 : (h + 1) * 128] * tiled[
-                        rows, tile * 128 : (tile + 1) * 128
-                    ]
-                    acc = term if acc is None else acc + term
-                sums[:, t * step + h * 128 : t * step + (h + 1) * 128] = acc
-        whole = sums[...]
-        high = whole.astype(BF16)
-        low = (whole - high.astype(F32)).astype(BF16)
-        res = dot(high, fold[...]) + dot(low, fold[...])
-        wide = jnp.concatenate([res, jnp.zeros((leaves, expan.shape[1] - 128), F32)], axis=1)
-        expan[...] += pltpu.roll(wide, b * per_block, 1)
-
-    expansion = expan[...][:, :width].astype(BF16)
+    blocks = width * width // block
+    joint = 3 if blocks % 3 == 0 else 1
+
+    @pl.loop(0, blocks // joint)
+    def _(turn):
+        for k in range(joint):
+            table_copy(turn * joint + k).wait()
+        for k in range(joint):
+            b = turn * joint + k
+            lines = pl.ds(pl.multiple_of(b * leaves, leaves), leaves)
+            for t in range(block // step):
+                start = pl.multiple_of(b * block + t * step, 128)
+                oper = dot(hot_class[...], table[:, pl.ds(start, step)])
+                for h in range(step // 128):
+                    tile = ((t * step) // 128 + h) % (period // 128)
+                    acc = None
+                    for s in range(far_num):
+                        rows = slice(s * leaves, (s + 1) * leaves)
+                        term = oper[rows, h * 128 : (h + 1) * 128] * tiled[
+                            rows, tile * 128 : (tile + 1) * 128
+                        ]
+                        acc = term if acc is None else acc + term
+                    sums[lines, t * step + h * 128 : t * step + (h + 1) * 128] = acc
+
+    whole = sums[...]
+    high = whole.astype(BF16)
+    low = (whole - high.astype(F32)).astype(BF16)
+    res = dot(high, fold[...]) + dot(low, fold[...])
+    wide = jnp.zeros((leaves, expan_width), F32)
+    for b in range(blocks):
+        one = jnp.concatenate(
+            [res[b * leaves : (b + 1) * leaves], jnp.zeros((leaves, expan_width - 128), F32)], axis=1
+        )
+        wide = wide + (pltpu.roll(one, b * per_block, 1) if b else one)
+    expansion = wide[:, :width]
     get_down.wait()
-    leaf_row = iota((leaves, size), 0)
+    leaf_row = iota((leaves, width), 0)
+    nothing = jnp.zeros_like(expansion)
+    single = [
+        jnp.where(leaf_row == leaf, expansion, nothing).astype(BF16) for leaf in range(leaves)
+    ]
     for q in range(9):
-        field[q] = jnp.zeros((leaves, size), F32)
-
-    @pl.loop(0, leaves)
-    def _(leaf):
-        for q in range(9):
-            got = dot(expansion, down[leaf, q])
-            field[q] += jnp.where(leaf_row == leaf, got, 0.0)
+        total = None
+        for leaf in range(leaves):
+            got = dot(single[leaf], down[leaf, q])
+            total = got if total is None else total + got
+        field[q] = total
 
     @pl.when(has_right)
     def _():
@@ -627,9 +655,11 @@
             pltpu.VMEM((far_num * leaves, classes), BF16),
             pltpu.VMEM((far_num * leaves, cap * n), BF16),
             pltpu.VMEM((far_num * leaves, period), F32),
-            pltpu.VMEM((leaves, block), F32),
+            pltpu.VMEM((blocks * leaves, block), F32),
             pltpu.VMEM((block, 128), BF16),
-            pltpu.VMEM((leaves, (width + 127) // 128 * 128), F32),
+            pltpu.VMEM((128, leaves * slots), BF16),
+            pltpu.VMEM((cap * n, n * leaves), BF16),
+            pltpu.VMEM((width, period), BF16),
             pltpu.VMEM((12, leaves, size), F32),
             pltpu.SemaphoreType.DMA,
             pltpu.SemaphoreType.DMA((blocks,)),

time: 51.5 us -> 36.9 us (0.72)
  Pallas kernels: 49.9 us -> 35.3 us
    pallas_call x1, Pallas kernels: 49.9 us -> 35.3 us  [per_device(): pl.pallas_call(functools.partial(body, n), out_shape=jax.ShapeDtypeStruct...]
where the time goes in v2:
time: 36.9 us; the launch traced here: 36.6 us
  Pallas kernels  35.3 us (96%)
  local copies, waits for them, and re-layouts  1.38 us (4%)
    pallas_call x1, Pallas kernels, per_device(): pl.pallas_call(functools.partial(body, n), out_shape=jax.ShapeDtypeStruct...  35.3 us
    unnamed x1, local copies, waits for them, and re-layouts  1.38 us

profile of v2, /device:TPU:0, one launch (start us, length us, event | category | flops | bytes accessed | tf_op | source)
XLA Modules:
  0.0 36.6 jit_solution(17166763883613610071)
XLA Ops:
  0.0 35.3 %shard_map.127 = f32[3,2048]{1,0:T(4,128)} custom-call(s32[8,16]{1,0:T(8,128)} %bitcast.6, s32[16]{0:T(128)} %near_count.1, s32[16]{0:T(128)} %far_count.1, f32[3,2048]{1,0:T(4,128)} %pos.1, f32[3,2048]{1,0:T(4,128)} %dens.1, s32[16,32]{1,0:T(8,128)} %far_slot.1, s32[16,32]{1,0:T(8,128)} %far_class.1, s32[4,32]{1,0:T(4,128)} %bitcast.7, ...), custom_call_target="tpu_custom_call" | custom-call | tf_op jit(solution)/shard_map/pallas_call | solution.py:627
  35.3 1.4 %copy.15 = f32[3,2048]{1,0:T(4,128)} copy(f32[3,2048]{1,0:T(4,128)} %shard_map.127) | data formatting | bytes 49152

commit v3 on v2

--- a/solution.py
+++ b/solution.py
@@ -113,6 +113,20 @@
 
 def body(
     n,
+    near_src_hbm,
+    near_count_hbm,
+    far_count_hbm,
+    pos_hbm,
+    dens_hbm,
+    far_slot_hbm,
+    far_class_hbm,
+    req_hbm,
+    choose_src_hbm,
+    choose_tgt_hbm,
+    up_hbm,
+    table_hbm,
+    down_hbm,
+    out,
     near_src,
     near_count,
     far_count,
@@ -123,10 +137,6 @@
     req,
     choose_src,
     choose_tgt,
-    up_hbm,
-    table_hbm,
-    down_hbm,
-    out,
     pos_b,
     pos_a,
     dens_b,
@@ -154,6 +164,7 @@
     got_a,
     hot_class,
     hot_slot,
+    ready,
     tiled,
     sums,
     fold,
@@ -161,6 +172,7 @@
     pick,
     spread,
     field,
+    in_sem,
     up_sem,
     table_sem,
     down_sem,
@@ -200,6 +212,25 @@
     def _():
         signal(me + 1)
 
+    ins = [
+        pltpu.make_async_copy(src, dst, in_sem.at[k])
+        for k, (src, dst) in enumerate(
+            (
+                (pos_hbm, pos),
+                (dens_hbm, dens),
+                (choose_tgt_hbm, choose_tgt),
+                (near_src_hbm, near_src),
+                (near_count_hbm, near_count),
+                (far_count_hbm, far_count),
+                (far_slot_hbm, far_slot),
+                (far_class_hbm, far_class),
+                (req_hbm, req),
+                (choose_src_hbm, choose_src),
+            )
+        )
+    ]
+    for copy in ins:
+        copy.start()
     get_up = pltpu.make_async_copy(up_hbm, up, up_sem)
     get_up.start()
 
@@ -209,26 +240,9 @@
             table_hbm.at[:, lanes], table.at[:, lanes], table_sem.at[b]
         )
 
-    for b in range(width * width // block):
-        table_copy(b).start()
     get_down = pltpu.make_async_copy(down_hbm, down, down_sem)
-    get_down.start()
-
-    for leaf in range(leaves):
-        for c in range(3):
-            dens_rows[leaf : leaf + 1, c * size : (c + 1) * size] = dens[
-                c : c + 1, leaf * size : (leaf + 1) * size
-            ]
-    dens_round = dens_rows[...].astype(BF16)
-    get_up.wait()
-    row = iota((leaves, width), 0)
-    total = jnp.zeros((leaves, width), F32)
-    for leaf in range(leaves):
-        got = lax.dot_general(
-            dens_round, up[leaf], (((1,), (1,)), ((), ())), preferred_element_type=F32
-        )
-        total = total + jnp.where(row == leaf, got, 0.0)
-    mom[0] = total.astype(BF16)
+    for copy in ins:
+        copy.wait()
 
     def halo(k, src, dst, peer):
         return pltpu.make_async_remote_copy(
@@ -253,6 +267,25 @@
             device_id_type=MESH,
         )
 
+    for leaf in range(leaves):
+        for c in range(3):
+            dens_rows[leaf : leaf + 1, c * size : (c + 1) * size] = dens[
+                c : c + 1, leaf * size : (leaf + 1) * size
+            ]
+    dens_round = dens_rows[...].astype(BF16)
+    get_up.wait()
+    for b in range(width * width // block):
+        table_copy(b).start()
+    get_down.start()
+    row = iota((leaves, width), 0)
+    total = jnp.zeros((leaves, width), F32)
+    for leaf in range(leaves):
+        got = lax.dot_general(
+            dens_round, up[leaf], (((1,), (1,)), ((), ())), preferred_element_type=F32
+        )
+        total = total + jnp.where(row == leaf, got, 0.0)
+    mom[0] = total.astype(BF16)
+
     pl.semaphore_wait(
         barrier, phases + has_left.astype(jnp.int32) + has_right.astype(jnp.int32)
     )
@@ -266,6 +299,7 @@
     def _():
         for copy in to_left:
             copy.start()
+
 
     gather(0).start()
 
@@ -394,13 +428,18 @@
 
     sources(2, rows_own, pos_a, dens_a)
 
+    group = 1
+    steps = slots // group
+    together = 4
+
     def geometry(geo, leaf, first):
-        for k in range(2):
+        for k in range(group):
             geo[k] = dot(lhs[leaf][:, :FEATURES], rhs[source_of(leaf, first + k)])
 
+    step = 256 if block % 256 == 0 else 128
+    per_block = block // width
+    blocks = width * width // block
     geometry(geo0, 0, 0)
-    pairs = slots // 2
-    together = 2
 
     @pl.loop(0, leaves // together)
     def _(turn):
@@ -410,18 +449,24 @@
                 gather(t - 1).wait_recv()
                 gather(t).start()
 
-        for sub in range(together * pairs):
-            leaf = turn * together + sub // pairs
-            pair = sub % pairs
-            following = lax.rem(leaf + 1, leaves)
-            geo, other = ((geo0, geo1), (geo1, geo0))[pair % 2]
-            if pair + 1 < pairs:
-                geometry(other, leaf, 2 * pair + 2)
+        table_copy(turn).wait()
+        for sub in range(together * steps):
+            leaf = turn * together + sub // steps
+            step_now = sub % steps
+            geo, other = ((geo0, geo1), (geo1, geo0))[sub % 2]
+            if sub + 1 < together * steps:
+                nxt = sub + 1
+                geometry(other, turn * together + nxt // steps, group * (nxt % steps))
             else:
-                geometry(other, following, 0)
+                geometry(other, lax.rem((turn + 1) * together, leaves), 0)
+            if sub % 3 == 0 and sub // 3 < block // step:
+                start = pl.multiple_of(turn * block + (sub // 3) * step, 128)
+                ready[turn, :, (sub // 3) * step : (sub // 3 + 1) * step] = dot(
+                    hot_class[...], table[:, pl.ds(start, step)]
+                )
             xs, fs, sums_src = [], [], []
-            for k in range(2):
-                index = source_of(leaf, 2 * pair + k)
+            for k in range(group):
+                index = source_of(leaf, group * step_now + k)
                 nodes_k = window[index]
                 xs.append([jnp.broadcast_to(nodes_k[c : c + 1], (8, size)) for c in range(3)])
                 fs.append([jnp.broadcast_to(nodes_k[3 + c : 4 + c], (8, size)) for c in range(3)])
@@ -429,7 +474,7 @@
             for g in range(size // 8):
                 r8 = slice(g * 8, (g + 1) * 8)
                 total = [None] * 3
-                for k in range(2):
+                for k in range(group):
                     ab, ar, br, rho = [
                         geo[k, r8, o * size : (o + 1) * size] for o in range(4)
                     ]
@@ -446,17 +491,18 @@
                         sums_src[k][c] = term if g == 0 else sums_src[k][c] + term
                         total[c] = term if k == 0 else total[c] + term
                 for c in range(3):
-                    if pair > 0:
+                    if step_now > 0:
                         total[c] = total[c] + tacc[c, r8, :]
-                    if pair + 1 < pairs:
+                    if step_now + 1 < steps:
                         tacc[c, r8, :] = total[c]
                     else:
                         col = jnp.sum(total[c], axis=1, keepdims=True)
                         cols[r8, :] = jnp.where(lane8 == c * leaves + leaf, col, cols[r8, :])
-            for k in range(2):
+            for k in range(group):
+                at_k = group * step_now + k
                 for c in range(3):
-                    src_rows[leaf, 2 * pair + k : 2 * pair + k + 1, c * size : (c + 1) * size] = (
-                        jnp.sum(sums_src[k][c], axis=0, keepdims=True)
+                    src_rows[leaf, at_k : at_k + 1, c * size : (c + 1) * size] = jnp.sum(
+                        sums_src[k][c], axis=0, keepdims=True
                     )
 
     near_t = jnp.transpose(cols[...])
@@ -502,31 +548,45 @@
     chosen_rows = dot(chosen, spread[...]).astype(BF16)
     tiled[...] = dot(hot_slot[...], chosen_rows)
 
-    step = 256 if block % 256 == 0 else 128
-    per_block = block // width
-    blocks = width * width // block
-    joint = 3 if blocks % 3 == 0 else 1
-
-    @pl.loop(0, blocks // joint)
-    def _(turn):
-        for k in range(joint):
-            table_copy(turn * joint + k).wait()
-        for k in range(joint):
-            b = turn * joint + k
-            lines = pl.ds(pl.multiple_of(b * leaves, leaves), leaves)
-            for t in range(block // step):
-                start = pl.multiple_of(b * block + t * step, 128)
-                oper = dot(hot_class[...], table[:, pl.ds(start, step)])
-                for h in range(step // 128):
-                    tile = ((t * step) // 128 + h) % (period // 128)
-                    acc = None
-                    for s in range(far_num):
-                        rows = slice(s * leaves, (s + 1) * leaves)
-                        term = oper[rows, h * 128 : (h + 1) * 128] * tiled[
-                            rows, tile * 128 : (tile + 1) * 128
-                        ]
-                        acc = term if acc is None else acc + term
-                    sums[lines, t * step + h * 128 : t * step + (h + 1) * 128] = acc
+
+    early = ready.shape[0]
+
+    def apply(members, t):
+        for h in range(step // 128):
+            tile = ((t * step) // 128 + h) % (period // 128)
+            acc = [None] * len(members)
+            for s in range(far_num):
+                rows = slice(s * leaves, (s + 1) * leaves)
+                factor = tiled[rows, tile * 128 : (tile + 1) * 128]
+                for k, (b, oper) in enumerate(members):
+                    term = oper(rows, h) * factor
+                    acc[k] = term if acc[k] is None else acc[k] + term
+            for k, (b, oper) in enumerate(members):
+                lines = pl.ds(pl.multiple_of(b * leaves, leaves), leaves)
+                sums[lines, t * step + h * 128 : t * step + (h + 1) * 128] = acc[k]
+
+    def fresh(b, t):
+        start = pl.multiple_of(b * block + t * step, 128)
+        oper = dot(hot_class[...], table[:, pl.ds(start, step)])
+        return b, lambda rows, h: oper[rows, h * 128 : (h + 1) * 128]
+
+    def stored(b, t):
+        return b, lambda rows, h: ready[
+            b, rows, t * step + h * 128 : t * step + (h + 1) * 128
+        ]
+
+    paired = min(early, blocks - early)
+
+    @pl.loop(0, paired)
+    def _(b):
+        table_copy(early + b).wait()
+        for t in range(block // step):
+            apply((fresh(early + b, t), stored(b, t)), t)
+
+    for b in range(early + paired, blocks):
+        table_copy(b).wait()
+        for t in range(block // step):
+            apply((fresh(b, t),), t)
 
     whole = sums[...]
     high = whole.astype(BF16)
@@ -619,17 +679,28 @@
     block = 2 * period if blocks % 2 == 0 else period
     down = jnp.transpose(down_basis, (0, 2, 1, 3))
     blocks = width * width // block
-    smem = pl.BlockSpec(memory_space=pltpu.SMEM)
     vmem = pl.BlockSpec(memory_space=pltpu.VMEM)
     hbm = pl.BlockSpec(memory_space=pl.ANY)
     line = pltpu.VMEM((3, nodes), F32)
     part = pltpu.VMEM((leaves, 3 * size), F32)
     return pl.pallas_call(
         functools.partial(body, n),
-        out_shape=jax.ShapeDtypeStruct((3, nodes), F32),
-        in_specs=[smem] * 3 + [vmem] * 7 + [hbm] * 3,
+        out_shape=pltpu.VMEM((3, nodes), F32),
+        in_specs=[hbm] * 13,
         out_specs=vmem,
-        scratch_shapes=[line] * 4
+        scratch_shapes=[
+            pltpu.SMEM((slots, leaves), jnp.int32),
+            pltpu.SMEM((leaves,), jnp.int32),
+            pltpu.SMEM((leaves,), jnp.int32),
+            line,
+            line,
+            pltpu.VMEM(far_slot.shape, jnp.int32),
+            pltpu.VMEM(far_class.shape, jnp.int32),
+            pltpu.VMEM((cap, n), jnp.int32),
+            pltpu.VMEM((4 * FEATURES, ROWS), BF16),
+            pltpu.VMEM((ROWS, 128 + 6 * size), BF16),
+        ]
+        + [line] * 4
         + [
             pltpu.VMEM(up_basis.shape, BF16),
             pltpu.VMEM(transfer_table.shape, BF16),
@@ -654,6 +725,7 @@
             part,
             pltpu.VMEM((far_num * leaves, classes), BF16),
             pltpu.VMEM((far_num * leaves, cap * n), BF16),
+            pltpu.VMEM((leaves // 4, far_num * leaves, block), F32),
             pltpu.VMEM((far_num * leaves, period), F32),
             pltpu.VMEM((blocks * leaves, block), F32),
             pltpu.VMEM((block, 128), BF16),
@@ -661,6 +733,7 @@
             pltpu.VMEM((cap * n, n * leaves), BF16),
             pltpu.VMEM((width, period), BF16),
             pltpu.VMEM((12, leaves, size), F32),
+            pltpu.SemaphoreType.DMA((10,)),
             pltpu.SemaphoreType.DMA,
             pltpu.SemaphoreType.DMA((blocks,)),
             pltpu.SemaphoreType.DMA,

time: 36.9 us -> 30.8 us (0.83)
  Pallas kernels: 35.3 us -> 30 us
  local copies, waits for them, and re-layouts: 1.38 us -> 0.62 us
    pallas_call x1, Pallas kernels: 35.3 us -> 30 us  [per_device(): pl.pallas_call(functools.partial(body, n), out_shape=pltpu.VMEM((3, nodes...]
    unnamed x1, local copies, waits for them, and re-layouts: 1.38 us -> 0.62 us
where the time goes in v3:
time: 30.8 us; the launch traced here: 30.6 us
  Pallas kernels  30 us (97%)
  local copies, waits for them, and re-layouts  0.62 us (2%)
    pallas_call x1, Pallas kernels, per_device(): pl.pallas_call(functools.partial(body, n), out_shape=pltpu.VMEM((3, nodes...  30 us
    unnamed x1, local copies, waits for them, and re-layouts  0.62 us

profile of v3, /device:TPU:0, one launch (start us, length us, event | category | flops | bytes accessed | tf_op | source)
XLA Modules:
  0.0 30.6 jit_solution(14910874688889926969)
XLA Ops:
  0.0 30.0 %shard_map.127 = f32[3,2048]{1,0:T(4,128)S(1)} custom-call(s32[8,16]{1,0:T(8,128)} %bitcast.6, s32[16]{0:T(128)} %near_count_hbm.1, s32[16]{0:T(128)} %far_count_hbm.1, f32[3,2048]{1,0:T(4,128)} %pos_hbm.1, f32[3,2048]{1,0:T(4,128)} %dens_hbm.1, s32[16,32]{1,0:T(8,128)} %far_slot_hbm.1, s32[16,32]{1,0:T(8,128)} %far_class_hbm.1, s32[4,32]{1,0:T(4,128)} %bitcast.7, ...), custom_call_target="tpu_custom_call" | custom-call | tf_op jit(solution)/shard_map/pallas_call | solution.py:686
  30.0 0.6 %copy.15 = f32[3,2048]{1,0:T(4,128)} copy(f32[3,2048]{1,0:T(4,128)S(1)} %shard_map.127) | data formatting | bytes 49152
